TPU v7x, 32 devices: a whole 2x2x4 slice. The times are simulated.
32 devices in a mesh: chain: 2 (over y), gz: 4 (over z), gy: 2 (over x), pa: 2 (over core).
Axes of the slice: x: 2, y: 2, z: 4, core: 2. Of those that a mesh axis runs over, the one named last changes fastest.
Arguments:
- probes: float32 [32, 32, 64, 256], P(('chain', 'pa'), 'gz', 'gy'), parts along dimension 0, may hold values from -6 to 6
- velocity: float32 [3, 64, 64, 256], P(None, ('chain', 'gz'), 'gy'), parts along dimension 1, may hold values from -0.3 to 0.3
- prior_scale: float32 [64, 64, 256], P(('chain', 'gz'), 'gy'), parts along dimension 0, may hold values from 0.3 to 3
- noise_precision: float32 [64, 64, 256], P(('chain', 'gz'), 'gy'), parts along dimension 0, may hold values from 0.3 to 3
- source_mask: int32 [64, 64, 256], P(('chain', 'gz'), 'gy'), parts along dimension 0, may hold values 0 or 1
- sensor_mask: int32 [64, 64, 256], P(('chain', 'gz'), 'gy'), parts along dimension 0, may hold values 0 or 1
Outputs:
- hessian: float32 [32, 32, 64, 256], P(('chain', 'pa'), 'gz', 'gy'), parts along dimension 0
- gram: float32 [32, 16], P(('chain', 'pa')), parts along dimension 0
There are 2 independent parts, one for each index of `chain`. A program takes and returns all parts, laid end to end along the dimension named above; each array names one. Nothing has to cross between parts.
All inputs are finite; a program needn't handle non-finite values. No bound on the sum of `source_mask` or of `sensor_mask` on one device may be relied on, other than what follows from the above.
Results may differ from a plain program's by a relative error of at most 0.0003.
Values sent between devices are 32-bit elements; how exact they have to be, the bound alone decides.
A program may use at most 128 MiB of HBM per device.

v0:
```python
import functools

import jax
import jax.numpy as jnp
import numpy as np
from jax import lax
from jax.experimental import pallas as pl
from jax.experimental.pallas import tpu as pltpu
from jax.sharding import PartitionSpec as P

STEPS = 5
diffuse_cross = 0.15
diffuse_along = 16.0
SENDS = 2 * (STEPS - 1)
F32 = jnp.float32
BF16 = jnp.bfloat16


def matrix_parts(length):
    banded = (1.0 + 2.0 * diffuse_along) * np.eye(length) - diffuse_along * (
        np.eye(length, k=1) + np.eye(length, k=-1)
    )
    matrix = np.linalg.inv(banded)
    high = matrix.astype(BF16)
    low = (matrix - high.astype(np.float64)).astype(BF16)
    return high, low


def kernel(
    sizes,
    probes_hbm,
    vel,
    prior,
    noise,
    smask,
    omask,
    mhigh,
    mlow,
    hess_hbm,
    gram_ref,
    own,
    other,
    states,
    field,
    grad,
    half,
    wsrc,
    wobs,
    xhigh,
    xlow,
    zsend,
    zrecv,
    ysend,
    yrecv,
    gpart,
    gtile,
    grecv,
    stile,
    srecv,
    send_sem,
    recv_sem,
    load_sem,
    store_sem,
    pair_send,
    pair_recv,
    g_send,
    g_recv,
    s_send,
    s_recv,
):
    ngz, ngy, npa = sizes
    np_, nz, ny, nx = own.shape
    gz, gy, pa = lax.axis_index("gz"), lax.axis_index("gy"), lax.axis_index("pa")
    has_to = (gz < ngz - 1, gz > 0, gy < ngy - 1, gy > 0)
    has_from = (gz > 0, gz < ngz - 1, gy > 0, gy < ngy - 1)
    target = ({"gz": gz + 1}, {"gz": gz - 1}, {"gy": gy + 1}, {"gy": gy - 1})

    plane = [(dy, dp) for dy in range(ngy) for dp in range(npa) if dy or dp]

    def plane_id(dy, dp):
        return {"gy": lax.rem(gy + dy, ngy), "pa": lax.rem(pa + dp, npa)}

    def line_id(dz):
        return {"gz": lax.rem(gz + dz, ngz)}

    def load(p):
        return pltpu.make_async_copy(probes_hbm.at[p], own.at[p], load_sem.at[p])

    for p in range(np_):
        load(p).start()

    barrier = pltpu.get_barrier_semaphore()
    peers = [plane_id(dy, dp) for dy, dp in plane] + [line_id(dz) for dz in range(1, ngz)]
    for peer in peers:
        pl.semaphore_signal(barrier, inc=1, device_id=peer, device_id_type=pl.DeviceIdType.MESH)

    def prepare(z, carry):
        half[0, z] = 0.5 * vel[0, z]
        half[1, z] = 0.5 * vel[1, z]
        half[2, z] = 0.5 * vel[2, z]
        wsrc[z] = smask[z].astype(F32) * prior[z]
        wobs[z] = omask[z].astype(F32) * noise[z]
        return carry

    lax.fori_loop(0, nz, prepare, 0)

    @pl.when(jnp.logical_not(has_from[0]))
    def _():
        zrecv[:, :, 0] = jnp.zeros((2, np_, ny, nx), F32)

    @pl.when(jnp.logical_not(has_from[1]))
    def _():
        zrecv[:, :, 1] = jnp.zeros((2, np_, ny, nx), F32)

    @pl.when(jnp.logical_not(has_from[2]))
    def _():
        yrecv[:, :, 0] = jnp.zeros((2, np_, nz, nx), F32)

    @pl.when(jnp.logical_not(has_from[3]))
    def _():
        yrecv[:, :, 1] = jnp.zeros((2, np_, nz, nx), F32)

    pl.semaphore_wait(barrier, len(peers))

    def pair_copy(dp):
        return pltpu.make_async_remote_copy(
            src_ref=probes_hbm,
            dst_ref=other.at[dp - 1],
            send_sem=pair_send.at[dp - 1],
            recv_sem=pair_recv.at[dp - 1],
            device_id={"pa": lax.rem(pa + npa - dp, npa)},
            device_id_type=pl.DeviceIdType.MESH,
        )

    for dp in range(1, npa):
        pair_copy(dp).start()

    def face(d, par, p):
        send, recv = (zsend, zrecv) if d < 2 else (ysend, yrecv)
        return pltpu.make_async_remote_copy(
            src_ref=send.at[par, p, d % 2],
            dst_ref=recv.at[par, p, d % 2],
            send_sem=send_sem.at[d, par, p],
            recv_sem=recv_sem.at[d, par, p],
            device_id=target[d],
            device_id_type=pl.DeviceIdType.MESH,
        )

    def await_sent(par, p, also=None):
        for d in range(4):
            cond = has_to[d] if also is None else jnp.logical_and(has_to[d], also)

            @pl.when(cond)
            def _():
                face(d, par, p).wait_send()

    def start_faces(par, p):
        for d in range(4):

            @pl.when(has_to[d])
            def _():
                face(d, par, p).start()

    def await_faces(par, p):
        for d in range(4):

            @pl.when(has_from[d])
            def _():
                face(d, par, p).wait_recv()

    row = lax.broadcasted_iota(jnp.int32, (ny, nx), 0)
    lane = lax.broadcasted_iota(jnp.int32, (ny, nx), 1)

    def from_below_y(value, edge):
        return jnp.where(row == 0, edge, pltpu.roll(value, 1, 0))

    def from_above_y(value, edge):
        return jnp.where(row == ny - 1, edge, pltpu.roll(value, ny - 1, 0))

    def from_below_x(value):
        return jnp.where(lane == 0, 0.0, pltpu.roll(value, 1, 1))

    def from_above_x(value):
        return jnp.where(lane == nx - 1, 0.0, pltpu.roll(value, nx - 1, 1))

    def put(z, value):
        high = value.astype(BF16)
        xhigh[z * ny : (z + 1) * ny] = high
        xlow[z * ny : (z + 1) * ny] = (value - high.astype(F32)).astype(BF16)

    def implicit():
        total = jnp.dot(xhigh[...], mhigh[...], preferred_element_type=F32)
        total += jnp.dot(xlow[...], mhigh[...], preferred_element_type=F32)
        total += jnp.dot(xhigh[...], mlow[...], preferred_element_type=F32)
        return total.reshape(nz, ny, nx)

    def send_state(n, par, p):
        zsend[par, p, 0] = states[n, p, nz - 1]
        zsend[par, p, 1] = states[n, p, 0]
        for z in range(nz):
            ysend[par, p, 0, z : z + 1] = states[n, p, z, ny - 1 : ny]
            ysend[par, p, 1, z : z + 1] = states[n, p, z, 0:1]
        start_faces(par, p)

    def send_field(par, p):
        zsend[par, p, 0] = (diffuse_cross - half[2, nz - 1]) * field[p, nz - 1]
        zsend[par, p, 1] = (diffuse_cross + half[2, 0]) * field[p, 0]
        for z in range(nz):
            ysend[par, p, 0, z : z + 1] = (diffuse_cross - half[1, z, ny - 1 : ny]) * field[
                p, z, ny - 1 : ny
            ]
            ysend[par, p, 1, z : z + 1] = (diffuse_cross + half[1, z, 0:1]) * field[p, z, 0:1]
        start_faces(par, p)

    def forward(n, par, p):
        await_faces(par, p)
        for z in range(nz):
            centre = states[n, p, z]
            minus_z = states[n, p, z - 1] if z > 0 else zrecv[par, p, 0]
            plus_z = states[n, p, z + 1] if z < nz - 1 else zrecv[par, p, 1]
            minus_y = from_below_y(centre, yrecv[par, p, 0, z : z + 1])
            plus_y = from_above_y(centre, yrecv[par, p, 1, z : z + 1])
            drift = half[0, z] * (from_above_x(centre) - from_below_x(centre))
            drift += half[1, z] * (plus_y - minus_y) + half[2, z] * (plus_z - minus_z)
            cross = (plus_z + minus_z) + (plus_y + minus_y)
            moved = (1.0 - 4.0 * diffuse_cross) * centre + diffuse_cross * cross - drift
            put(z, moved + wsrc[z] * own[p, z])
        return implicit()

    def adjoint(n, par, p):
        await_faces(par, p)

        def split_z(z):
            value = field[p, z]
            flux = half[2, z] * value
            value = diffuse_cross * value
            return value + flux, value - flux

        below = zrecv[par, p, 0]
        here = split_z(0)
        for z in range(nz):
            above = split_z(z + 1) if z < nz - 1 else (zrecv[par, p, 1], None)
            centre = field[p, z]
            scaled = diffuse_cross * centre
            flux_y = half[1, z] * centre
            flux_x = half[0, z] * centre
            total = (1.0 - 4.0 * diffuse_cross) * centre + wobs[z] * states[n, p, z]
            total += above[0] + below
            total += from_above_y(scaled + flux_y, yrecv[par, p, 1, z : z + 1])
            total += from_below_y(scaled - flux_y, yrecv[par, p, 0, z : z + 1])
            total += from_above_x(flux_x) - from_below_x(flux_x)
            put(z, total)
            below = here[1]
            here = above
        return implicit()

    def first(p, carry):
        load(p).wait()
        for z in range(nz):
            put(z, wsrc[z] * own[p, z])
        states[0, p] = implicit()
        send_state(0, 0, p)
        return carry

    lax.fori_loop(0, np_, first, 0)

    def forward_step(index, carry):
        n, p = index // np_, lax.rem(index, np_)
        par = lax.rem(n, 2)
        states[n + 1, p] = forward(n, par, p)
        await_sent(1 - par, p, n >= 1)
        send_state(n + 1, 1 - par, p)
        return carry

    lax.fori_loop(0, (STEPS - 2) * np_, forward_step, 0)

    def turn(p, carry):
        par = (STEPS - 2) % 2
        last = forward(STEPS - 2, par, p)
        for z in range(nz):
            put(z, wobs[z] * last[z])
        pulled = implicit()
        field[p] = pulled
        grad[p] = pulled
        await_sent(1 - par, p)
        send_field(1 - par, p)
        return carry

    lax.fori_loop(0, np_, turn, 0)

    def adjoint_step(index, carry):
        step, p = index // np_, lax.rem(index, np_)
        par = lax.rem(step + STEPS - 1, 2)
        pulled = adjoint(STEPS - 2 - step, par, p)
        field[p] = pulled
        grad[p] = grad[p] + pulled
        await_sent(1 - par, p)
        send_field(1 - par, p)
        return carry

    lax.fori_loop(0, (STEPS - 2) * np_, adjoint_step, 0)

    for dp in range(1, npa):
        pair_copy(dp).wait()

    def store(p):
        return pltpu.make_async_copy(grad.at[p], hess_hbm.at[p], store_sem.at[p])

    def fold(value):
        return functools.reduce(jnp.add, [value[y : y + 8] for y in range(0, ny, 8)])

    def finish(p, carry):
        pulled = adjoint(0, (SENDS - 1) % 2, p)
        grad[p] = wsrc[...] * (grad[p] + pulled)
        store(p).start()
        for dp in range(npa):
            sums = [None] * np_
            for z in range(nz):
                action = grad[p, z]
                for i in range(np_):
                    probe = own[i, z] if dp == 0 else other[dp - 1, i, z]
                    term = fold(probe * action)
                    sums[i] = term if sums[i] is None else sums[i] + term
            for i in range(np_):
                part = functools.reduce(
                    jnp.add, [sums[i][:, x : x + 128] for x in range(0, nx, 128)]
                )
                gpart[dp, p, i : i + 1] = jnp.sum(part, axis=0, keepdims=True)
        return carry

    lax.fori_loop(0, np_, finish, 0)

    column = lax.broadcasted_iota(jnp.int32, (np_, 128), 1)
    for dp in range(npa):
        tile = jnp.zeros((np_, 128), F32)
        for j in range(np_):
            sums = jnp.sum(gpart[dp, j], axis=1, keepdims=True)
            tile = jnp.where(column == pa * np_ + j, sums, tile)
        gtile[dp] = tile

    def plane_copy(k):
        dy, dp = plane[k]
        return pltpu.make_async_remote_copy(
            src_ref=gtile.at[dp],
            dst_ref=grecv.at[k],
            send_sem=g_send.at[k],
            recv_sem=g_recv.at[k],
            device_id=plane_id(dy, dp),
            device_id_type=pl.DeviceIdType.MESH,
        )

    def line_copy(dz):
        return pltpu.make_async_remote_copy(
            src_ref=stile,
            dst_ref=srecv.at[dz - 1],
            send_sem=s_send.at[dz - 1],
            recv_sem=s_recv.at[dz - 1],
            device_id=line_id(dz),
            device_id_type=pl.DeviceIdType.MESH,
        )

    for k in range(len(plane)):
        plane_copy(k).start()
    total = gtile[0]
    for k in range(len(plane)):
        plane_copy(k).wait_recv()
        total += grecv[k]
    stile[...] = total
    for dz in range(1, ngz):
        line_copy(dz).start()
    for k in range(len(plane)):
        plane_copy(k).wait_send()

    def drain(p, carry):
        store(p).wait()
        await_sent(0, p)
        await_sent(1, p)
        return carry

    lax.fori_loop(0, np_, drain, 0)

    for dz in range(1, ngz):
        line_copy(dz).wait_recv()
        total += srecv[dz - 1]
    for dz in range(1, ngz):
        line_copy(dz).wait_send()
    cells = nz * ny * nx * ngz * ngy
    gram_ref[...] = total[:, : npa * np_] / cells


def shards(probes, velocity, prior_scale, noise_precision, source_mask, sensor_mask):
    np_, nz, ny, nx = probes.shape
    ngz, ngy, npa = lax.axis_size("gz"), lax.axis_size("gy"), lax.axis_size("pa")
    high, low = matrix_parts(nx)
    plane = ngy * npa - 1
    vmem = pl.BlockSpec(memory_space=pltpu.VMEM)
    hbm = pl.BlockSpec(memory_space=pl.ANY)
    dma = pltpu.SemaphoreType.DMA
    return pl.pallas_call(
        functools.partial(kernel, (ngz, ngy, npa)),
        out_shape=(
            jax.ShapeDtypeStruct(probes.shape, F32),
            jax.ShapeDtypeStruct((np_, npa * np_), F32),
        ),
        in_specs=[hbm] + [vmem] * 7,
        out_specs=(hbm, vmem),
        scratch_shapes=[
            pltpu.VMEM((np_, nz, ny, nx), F32),
            pltpu.VMEM((npa - 1, np_, nz, ny, nx), F32),
            pltpu.VMEM((STEPS - 1, np_, nz, ny, nx), F32),
            pltpu.VMEM((np_, nz, ny, nx), F32),
            pltpu.VMEM((np_, nz, ny, nx), F32),
            pltpu.VMEM((3, nz, ny, nx), F32),
            pltpu.VMEM((nz, ny, nx), F32),
            pltpu.VMEM((nz, ny, nx), F32),
            pltpu.VMEM((nz * ny, nx), BF16),
            pltpu.VMEM((nz * ny, nx), BF16),
            pltpu.VMEM((2, np_, 2, ny, nx), F32),
            pltpu.VMEM((2, np_, 2, ny, nx), F32),
            pltpu.VMEM((2, np_, 2, nz, nx), F32),
            pltpu.VMEM((2, np_, 2, nz, nx), F32),
            pltpu.VMEM((npa, np_, np_, 128), F32),
            pltpu.VMEM((npa, np_, 128), F32),
            pltpu.VMEM((plane, np_, 128), F32),
            pltpu.VMEM((np_, 128), F32),
            pltpu.VMEM((ngz - 1, np_, 128), F32),
            dma((4, 2, np_)),
            dma((4, 2, np_)),
            dma((np_,)),
            dma((np_,)),
            dma((npa - 1,)),
            dma((npa - 1,)),
            dma((plane,)),
            dma((plane,)),
            dma((ngz - 1,)),
            dma((ngz - 1,)),
        ],
        compiler_params=pltpu.CompilerParams(
            collective_id=0, has_side_effects=True, vmem_limit_bytes=48 * 1024 * 1024
        ),
    )(
        probes,
        velocity,
        prior_scale,
        noise_precision,
        source_mask,
        sensor_mask,
        jnp.asarray(high),
        jnp.asarray(low),
    )


def solution(mesh):
    in_specs = (
        P(("chain", "pa"), "gz", "gy", None),
        P(None, ("chain", "gz"), "gy", None),
        P(("chain", "gz"), "gy", None),
        P(("chain", "gz"), "gy", None),
        P(("chain", "gz"), "gy", None),
        P(("chain", "gz"), "gy", None),
    )
    out_specs = (P(("chain", "pa"), "gz", "gy", None), P(("chain", "pa"), None))
    return jax.shard_map(shards, mesh=mesh, in_specs=in_specs, out_specs=out_specs, check_vma=False)
```

profile of v0, /device:TPU:0, one launch (start us, length us, event | category | flops | bytes accessed | tf_op | source)
XLA Modules:
  0.0 71.0 jit_solution(7623058051027196582)
XLA Ops:
  0.6 0.0 copy-start
  0.6 1.1 %copy-done = f32[3,8,32,256]{3,2,1,0:T(8,128)S(1)} copy-done((f32[3,8,32,256]{3,2,1,0:T(8,128)S(1)}, f32[3,8,32,256]{3,2,1,0:T(8,128)}, u32[]{:S(2)}) %copy-start) | copy-done | bytes 786456
  1.8 0.0 copy-start.1
  1.8 0.9 %copy-done.1 = f32[8,32,256]{2,1,0:T(8,128)S(1)} copy-done((f32[8,32,256]{2,1,0:T(8,128)S(1)}, f32[8,32,256]{2,1,0:T(8,128)}, u32[]{:S(2)}) %copy-start.1) | copy-done | bytes 262168
  2.7 0.0 copy-start.2
  2.7 0.9 %copy-done.2 = f32[8,32,256]{2,1,0:T(8,128)S(1)} copy-done((f32[8,32,256]{2,1,0:T(8,128)S(1)}, f32[8,32,256]{2,1,0:T(8,128)}, u32[]{:S(2)}) %copy-start.2) | copy-done | bytes 262168
  3.7 0.0 copy-start.3
  3.7 0.9 %copy-done.3 = s32[8,32,256]{2,1,0:T(8,128)S(1)} copy-done((s32[8,32,256]{2,1,0:T(8,128)S(1)}, s32[8,32,256]{2,1,0:T(8,128)}, u32[]{:S(2)}) %copy-start.3) | copy-done | bytes 262168
  4.6 0.0 copy-start.4
  4.6 0.9 %copy-done.4 = s32[8,32,256]{2,1,0:T(8,128)S(1)} copy-done((s32[8,32,256]{2,1,0:T(8,128)S(1)}, s32[8,32,256]{2,1,0:T(8,128)}, u32[]{:S(2)}) %copy-start.4) | copy-done | bytes 262168
  5.6 0.0 copy-start.5
  5.6 0.9 %copy-done.5 = bf16[256,256]{1,0:T(8,128)(2,1)S(1)} copy-done((bf16[256,256]{1,0:T(8,128)(2,1)S(1)}, bf16[256,256]{1,0:T(8,128)(2,1)}, u32[]{:S(2)}) %copy-start.5) | copy-done | bytes 131096
  6.5 0.0 copy-start.6
  6.5 0.9 %copy-done.6 = bf16[256,256]{1,0:T(8,128)(2,1)S(1)} copy-done((bf16[256,256]{1,0:T(8,128)(2,1)S(1)}, bf16[256,256]{1,0:T(8,128)(2,1)}, u32[]{:S(2)}) %copy-start.6) | copy-done | bytes 131096
  7.4 61.7 %shard_map.95 = (f32[8,8,32,256]{3,2,1,0:T(8,128)S(1)}, f32[8,16]{1,0:T(8,128)S(1)}) custom-call(f32[8,8,32,256]{3,2,1,0:T(8,128)} %probes_hbm.1, f32[3,8,32,256]{3,2,1,0:T(8,128)S(1)} %copy-done, f32[8,32,256]{2,1,0:T(8,128)S(1)} %copy-done.1, f32[8,32,256]{2,1,0:T(8,128)S(1)} %copy-done.2, s32[8,32,256]{2,1,0:T(8,128)S(1)} %copy-done.3, ...), custom_call_target="tpu_custom_call" | custom-call | tf_op jit(solution)/shard_map/pallas_call | solution.py:399
  69.1 1.3 %copy.12 = f32[8,8,32,256]{3,2,1,0:T(8,128)} copy(f32[8,8,32,256]{3,2,1,0:T(8,128)S(1)} %get-tuple-element.4) | data formatting | bytes 4194304
  70.4 0.6 copy.13
Async XLA Ops:
  0.6 1.1 %copy-start = (f32[3,8,32,256]{3,2,1,0:T(8,128)S(1)}, f32[3,8,32,256]{3,2,1,0:T(8,128)}, u32[]{:S(2)}) copy-start(f32[3,8,32,256]{3,2,1,0:T(8,128)} %vel.1) | copy-start | bytes 2359300
  1.8 0.9 %copy-start.1 = (f32[8,32,256]{2,1,0:T(8,128)S(1)}, f32[8,32,256]{2,1,0:T(8,128)}, u32[]{:S(2)}) copy-start(f32[8,32,256]{2,1,0:T(8,128)} %prior.1) | copy-start | bytes 786436
  2.7 0.9 %copy-start.2 = (f32[8,32,256]{2,1,0:T(8,128)S(1)}, f32[8,32,256]{2,1,0:T(8,128)}, u32[]{:S(2)}) copy-start(f32[8,32,256]{2,1,0:T(8,128)} %noise.1) | copy-start | bytes 786436
  3.7 0.9 %copy-start.3 = (s32[8,32,256]{2,1,0:T(8,128)S(1)}, s32[8,32,256]{2,1,0:T(8,128)}, u32[]{:S(2)}) copy-start(s32[8,32,256]{2,1,0:T(8,128)} %smask.1) | copy-start | bytes 786436
  4.6 0.9 %copy-start.4 = (s32[8,32,256]{2,1,0:T(8,128)S(1)}, s32[8,32,256]{2,1,0:T(8,128)}, u32[]{:S(2)}) copy-start(s32[8,32,256]{2,1,0:T(8,128)} %omask.1) | copy-start | bytes 786436
  5.6 0.9 %copy-start.5 = (bf16[256,256]{1,0:T(8,128)(2,1)S(1)}, bf16[256,256]{1,0:T(8,128)(2,1)}, u32[]{:S(2)}) copy-start(bf16[256,256]{1,0:T(8,128)(2,1)} %constant.5.clone.mlow) | copy-start | bytes 393220
  6.5 0.9 %copy-start.6 = (bf16[256,256]{1,0:T(8,128)(2,1)S(1)}, bf16[256,256]{1,0:T(8,128)(2,1)}, u32[]{:S(2)}) copy-start(bf16[256,256]{1,0:T(8,128)(2,1)} %constant.4.clone.mhigh) | copy-start | bytes 393220
where the time goes:
time: 71.3 us; the launch traced here: 71 us
  Pallas kernels  61.7 us (87%)
  local copies, waits for them, and re-layouts  8.65 us (12%)
    pallas_call x1, Pallas kernels, shards(): pl.pallas_call(functools.partial(kernel, (ngz, ngy, npa)), out_shape=(jax...  61.7 us
    unnamed x16, local copies, waits for them, and re-layouts  8.65 us

commit v1 on v0

--- a/solution.py
+++ b/solution.py
@@ -29,13 +29,13 @@
 def kernel(
     sizes,
     probes_hbm,
-    vel,
-    prior,
-    noise,
-    smask,
-    omask,
-    mhigh,
-    mlow,
+    vel_hbm,
+    prior_hbm,
+    noise_hbm,
+    smask_hbm,
+    omask_hbm,
+    mhigh_hbm,
+    mlow_hbm,
     hess_hbm,
     gram_ref,
     own,
@@ -43,9 +43,14 @@
     states,
     field,
     grad,
+    moved2,
     half,
     wsrc,
     wobs,
+    smask,
+    omask,
+    mhigh,
+    mlow,
     xhigh,
     xlow,
     zsend,
@@ -60,6 +65,7 @@
     send_sem,
     recv_sem,
     load_sem,
+    coef_sem,
     store_sem,
     pair_send,
     pair_recv,
@@ -86,7 +92,26 @@
     def load(p):
         return pltpu.make_async_copy(probes_hbm.at[p], own.at[p], load_sem.at[p])
 
-    for p in range(np_):
+    coefs = [
+        (smask_hbm, smask),
+        (prior_hbm, wsrc),
+        (mhigh_hbm, mhigh),
+        (mlow_hbm, mlow),
+        (vel_hbm, half),
+        (omask_hbm, omask),
+        (noise_hbm, wobs),
+    ]
+
+    def coef(k):
+        return pltpu.make_async_copy(coefs[k][0], coefs[k][1], coef_sem.at[k])
+
+    for k in range(4):
+        coef(k).start()
+    load(0).start()
+    load(1).start()
+    for k in range(4, len(coefs)):
+        coef(k).start()
+    for p in range(2, np_):
         load(p).start()
 
     barrier = pltpu.get_barrier_semaphore()
@@ -94,16 +119,6 @@
     for peer in peers:
         pl.semaphore_signal(barrier, inc=1, device_id=peer, device_id_type=pl.DeviceIdType.MESH)
 
-    def prepare(z, carry):
-        half[0, z] = 0.5 * vel[0, z]
-        half[1, z] = 0.5 * vel[1, z]
-        half[2, z] = 0.5 * vel[2, z]
-        wsrc[z] = smask[z].astype(F32) * prior[z]
-        wobs[z] = omask[z].astype(F32) * noise[z]
-        return carry
-
-    lax.fori_loop(0, nz, prepare, 0)
-
     @pl.when(jnp.logical_not(has_from[0]))
     def _():
         zrecv[:, :, 0] = jnp.zeros((2, np_, ny, nx), F32)
@@ -120,20 +135,36 @@
     def _():
         yrecv[:, :, 1] = jnp.zeros((2, np_, nz, nx), F32)
 
+    for k in range(4):
+        coef(k).wait()
+
+    def prepare_source(z, carry):
+        wsrc[z] = smask[z].astype(F32) * wsrc[z]
+        return carry
+
+    lax.fori_loop(0, nz, prepare_source, 0)
+
     pl.semaphore_wait(barrier, len(peers))
 
-    def pair_copy(dp):
+    pair_sources = (probes_hbm, states.at[0], moved2)
+
+    def pair_copy(dp, k):
         return pltpu.make_async_remote_copy(
-            src_ref=probes_hbm,
-            dst_ref=other.at[dp - 1],
-            send_sem=pair_send.at[dp - 1],
-            recv_sem=pair_recv.at[dp - 1],
+            src_ref=pair_sources[k],
+            dst_ref=other.at[dp - 1, k],
+            send_sem=pair_send.at[dp - 1, k],
+            recv_sem=pair_recv.at[dp - 1, k],
             device_id={"pa": lax.rem(pa + npa - dp, npa)},
             device_id_type=pl.DeviceIdType.MESH,
         )
 
-    for dp in range(1, npa):
-        pair_copy(dp).start()
+    def start_pairs(k):
+        for dp in range(1, npa):
+            pair_copy(dp, k).start()
+
+    def await_pairs(k):
+        for dp in range(1, npa):
+            pair_copy(dp, k).wait()
 
     def face(d, par, p):
         send, recv = (zsend, zrecv) if d < 2 else (ysend, yrecv)
@@ -212,7 +243,7 @@
             ysend[par, p, 1, z : z + 1] = (diffuse_cross + half[1, z, 0:1]) * field[p, z, 0:1]
         start_faces(par, p)
 
-    def forward(n, par, p):
+    def forward(n, par, p, keep=False):
         await_faces(par, p)
         for z in range(nz):
             centre = states[n, p, z]
@@ -224,7 +255,10 @@
             drift += half[1, z] * (plus_y - minus_y) + half[2, z] * (plus_z - minus_z)
             cross = (plus_z + minus_z) + (plus_y + minus_y)
             moved = (1.0 - 4.0 * diffuse_cross) * centre + diffuse_cross * cross - drift
-            put(z, moved + wsrc[z] * own[p, z])
+            moved += wsrc[z] * own[p, z]
+            if keep:
+                moved2[p, z] = moved
+            put(z, moved)
         return implicit()
 
     def adjoint(n, par, p):
@@ -263,16 +297,37 @@
         return carry
 
     lax.fori_loop(0, np_, first, 0)
+    start_pairs(0)
+
+    for k in range(4, len(coefs)):
+        coef(k).wait()
+
+    def prepare(z, carry):
+        for k in range(3):
+            half[k, z] = 0.5 * half[k, z]
+        wobs[z] = omask[z].astype(F32) * wobs[z]
+        return carry
+
+    lax.fori_loop(0, nz, prepare, 0)
+
+    def second(p, carry):
+        states[1, p] = forward(0, 0, p, True)
+        send_state(1, 1, p)
+        return carry
+
+    lax.fori_loop(0, np_, second, 0)
+    start_pairs(1)
+    start_pairs(2)
 
     def forward_step(index, carry):
-        n, p = index // np_, lax.rem(index, np_)
+        n, p = index // np_ + 1, lax.rem(index, np_)
         par = lax.rem(n, 2)
         states[n + 1, p] = forward(n, par, p)
-        await_sent(1 - par, p, n >= 1)
+        await_sent(1 - par, p)
         send_state(n + 1, 1 - par, p)
         return carry
 
-    lax.fori_loop(0, (STEPS - 2) * np_, forward_step, 0)
+    lax.fori_loop(0, (STEPS - 3) * np_, forward_step, 0)
 
     def turn(p, carry):
         par = (STEPS - 2) % 2
@@ -288,47 +343,66 @@
 
     lax.fori_loop(0, np_, turn, 0)
 
-    def adjoint_step(index, carry):
-        step, p = index // np_, lax.rem(index, np_)
-        par = lax.rem(step + STEPS - 1, 2)
-        pulled = adjoint(STEPS - 2 - step, par, p)
-        field[p] = pulled
-        grad[p] = grad[p] + pulled
-        await_sent(1 - par, p)
-        send_field(1 - par, p)
-        return carry
-
-    lax.fori_loop(0, (STEPS - 2) * np_, adjoint_step, 0)
-
-    for dp in range(1, npa):
-        pair_copy(dp).wait()
-
-    def store(p):
-        return pltpu.make_async_copy(grad.at[p], hess_hbm.at[p], store_sem.at[p])
-
     def fold(value):
         return functools.reduce(jnp.add, [value[y : y + 8] for y in range(0, ny, 8)])
 
-    def finish(p, carry):
-        pulled = adjoint(0, (SENDS - 1) % 2, p)
-        grad[p] = wsrc[...] * (grad[p] + pulled)
-        store(p).start()
+    def gram_term(k, p, begin):
         for dp in range(npa):
             sums = [None] * np_
             for z in range(nz):
-                action = grad[p, z]
+                if k == 0:
+                    right = wsrc[z] * grad[p, z]
+                elif k == 1:
+                    right = wobs[z] * states[0, p, z]
+                else:
+                    right = field[p, z]
                 for i in range(np_):
-                    probe = own[i, z] if dp == 0 else other[dp - 1, i, z]
-                    term = fold(probe * action)
+                    if dp > 0:
+                        left = other[dp - 1, k, i, z]
+                    elif k == 0:
+                        left = own[i, z]
+                    elif k == 1:
+                        left = states[0, i, z]
+                    else:
+                        left = moved2[i, z]
+                    term = fold(left * right)
                     sums[i] = term if sums[i] is None else sums[i] + term
             for i in range(np_):
                 part = functools.reduce(
                     jnp.add, [sums[i][:, x : x + 128] for x in range(0, nx, 128)]
                 )
-                gpart[dp, p, i : i + 1] = jnp.sum(part, axis=0, keepdims=True)
-        return carry
-
-    lax.fori_loop(0, np_, finish, 0)
+                part = jnp.sum(part, axis=0, keepdims=True)
+                if not begin:
+                    part += gpart[dp, p, i : i + 1]
+                gpart[dp, p, i : i + 1] = part
+
+    for step in range(STEPS - 2):
+        par = (step + STEPS - 1) % 2
+        last = step == STEPS - 3
+        term = 2 if last else 0 if step == STEPS - 4 else 1 if step == 0 else None
+        if term is not None:
+            await_pairs(term)
+
+        def adjoint_step(p, carry):
+            pulled = adjoint(STEPS - 2 - step, par, p)
+            field[p] = pulled
+            grad[p] = grad[p] + pulled
+            await_sent(1 - par, p)
+            send_field(1 - par, p)
+            if term is not None:
+                gram_term(term, p, term == 1)
+            return carry
+
+        lax.fori_loop(0, np_, adjoint_step, 0)
+
+    def store(p):
+        return pltpu.make_async_copy(grad.at[p], hess_hbm.at[p], store_sem.at[p])
+
+    def finish(p, carry):
+        pulled = adjoint(0, (SENDS - 1) % 2, p)
+        grad[p] = wsrc[...] * (grad[p] + pulled)
+        store(p).start()
+        return carry
 
     column = lax.broadcasted_iota(jnp.int32, (np_, 128), 1)
     for dp in range(npa):
@@ -361,6 +435,7 @@
 
     for k in range(len(plane)):
         plane_copy(k).start()
+    lax.fori_loop(0, np_ // 4, finish, 0)
     total = gtile[0]
     for k in range(len(plane)):
         plane_copy(k).wait_recv()
@@ -370,6 +445,7 @@
         line_copy(dz).start()
     for k in range(len(plane)):
         plane_copy(k).wait_send()
+    lax.fori_loop(np_ // 4, np_, finish, 0)
 
     def drain(p, carry):
         store(p).wait()
@@ -379,6 +455,7 @@
 
     lax.fori_loop(0, np_, drain, 0)
 
+    total = stile[...]
     for dz in range(1, ngz):
         line_copy(dz).wait_recv()
         total += srecv[dz - 1]
@@ -402,17 +479,22 @@
             jax.ShapeDtypeStruct(probes.shape, F32),
             jax.ShapeDtypeStruct((np_, npa * np_), F32),
         ),
-        in_specs=[hbm] + [vmem] * 7,
+        in_specs=[hbm] * 8,
         out_specs=(hbm, vmem),
         scratch_shapes=[
             pltpu.VMEM((np_, nz, ny, nx), F32),
-            pltpu.VMEM((npa - 1, np_, nz, ny, nx), F32),
+            pltpu.VMEM((npa - 1, 3, np_, nz, ny, nx), F32),
             pltpu.VMEM((STEPS - 1, np_, nz, ny, nx), F32),
+            pltpu.VMEM((np_, nz, ny, nx), F32),
             pltpu.VMEM((np_, nz, ny, nx), F32),
             pltpu.VMEM((np_, nz, ny, nx), F32),
             pltpu.VMEM((3, nz, ny, nx), F32),
             pltpu.VMEM((nz, ny, nx), F32),
             pltpu.VMEM((nz, ny, nx), F32),
+            pltpu.VMEM((nz, ny, nx), jnp.int32),
+            pltpu.VMEM((nz, ny, nx), jnp.int32),
+            pltpu.VMEM((nx, nx), BF16),
+            pltpu.VMEM((nx, nx), BF16),
             pltpu.VMEM((nz * ny, nx), BF16),
             pltpu.VMEM((nz * ny, nx), BF16),
             pltpu.VMEM((2, np_, 2, ny, nx), F32),
@@ -427,16 +509,17 @@
             dma((4, 2, np_)),
             dma((4, 2, np_)),
             dma((np_,)),
+            dma((7,)),
             dma((np_,)),
-            dma((npa - 1,)),
-            dma((npa - 1,)),
+            dma((npa - 1, 3)),
+            dma((npa - 1, 3)),
             dma((plane,)),
             dma((plane,)),
             dma((ngz - 1,)),
             dma((ngz - 1,)),
         ],
         compiler_params=pltpu.CompilerParams(
-            collective_id=0, has_side_effects=True, vmem_limit_bytes=48 * 1024 * 1024
+            collective_id=0, has_side_effects=True, vmem_limit_bytes=62 * 1024 * 1024
         ),
     )(
         probes,

time: 71.3 us -> 65.2 us (0.914)
  local copies, waits for them, and re-layouts: 8.65 us -> 3.76 us
  Pallas kernels: 61.7 us -> 60.6 us
    unnamed x16 -> x4, local copies, waits for them, and re-layouts: 8.65 us -> 3.76 us
    pallas_call x1, Pallas kernels: 61.7 us -> 60.6 us  [shards(): pl.pallas_call(functools.partial(kernel, (ngz, ngy, npa)), out_shape=(jax...]
where the time goes in v1:
time: 65.2 us; the launch traced here: 65 us
  Pallas kernels  60.6 us (93%)
  local copies, waits for them, and re-layouts  3.76 us (6%)
    pallas_call x1, Pallas kernels, shards(): pl.pallas_call(functools.partial(kernel, (ngz, ngy, npa)), out_shape=(jax...  60.6 us
    unnamed x4, local copies, waits for them, and re-layouts  3.76 us

profile of v1, /device:TPU:0, one launch (start us, length us, event | category | flops | bytes accessed | tf_op | source)
XLA Modules:
  0.0 65.0 jit_solution(13439787557197390232)
XLA Ops:
  0.6 60.6 %shard_map.95 = (f32[8,8,32,256]{3,2,1,0:T(8,128)}, f32[8,16]{1,0:T(8,128)}) custom-call(f32[8,8,32,256]{3,2,1,0:T(8,128)} %probes_hbm.1, f32[3,8,32,256]{3,2,1,0:T(8,128)} %vel_hbm.1, f32[8,32,256]{2,1,0:T(8,128)} %prior_hbm.1, f32[8,32,256]{2,1,0:T(8,128)} %noise_hbm.1, s32[8,32,256]{2,1,0:T(8,128)} %smask_hbm.1, s32[8,32,256]{2,1,0:T(8,128)} %omask_hbm.1, ...), custom_call_target="tpu_custom_call" | custom-call | tf_op jit(solution)/shard_map/pallas_call | solution.py:476
  61.2 0.0 copy-start
  61.2 3.2 %copy.12 = f32[8,8,32,256]{3,2,1,0:T(8,128)} copy(f32[8,8,32,256]{3,2,1,0:T(8,128)} %get-tuple-element.4) | data formatting | bytes 4194304
  64.4 0.0 copy-done
  64.4 0.6 copy.13
Async XLA Ops:
  61.2 3.2 %copy-start = (f32[8,16]{1,0:T(8,128)S(1)}, f32[8,16]{1,0:T(8,128)}, u32[]{:S(2)}) copy-start(f32[8,16]{1,0:T(8,128)} %get-tuple-element.5) | copy-start | bytes 1540
